TPU v7x, 256 devices: a whole 4x4x8 slice. The times are simulated.
256 devices in a mesh: ctx: 32 (over x, z_lo, core), tp: 8 (over z_hi, y).
Axes of the slice: x: 4, y: 4, z: 8 (z_hi: 2, z_lo: 4; z = z_hi * 4 + z_lo), core: 2. Of those that a mesh axis runs over, the one named last changes fastest.
Arguments:
- token_ids: int32 [24576], P('ctx'), may hold values from 0 to 511
- embed_table: bfloat16 [512, 4096], replicated, may hold values from -6 to 6
- norm_gain: float32 [4096], replicated, may hold values from 0.25 to 1.75
- w_in: bfloat16 [4096, 3, 2048], P(None, None, 'tp'), may hold values from -0.09375 to 0.09375
- short_taps: float32 [3, 3, 2048], P(None, None, 'tp'), may hold values from -3 to 3
- long_filter: bfloat16 [2048, 24576], P('tp', 'ctx'), may hold values from -0.0390625 to 0.0390625
- skip_gain: float32 [2048], P('tp'), may hold values from 0.5 to 2
- w_out: bfloat16 [2048, 4096], P(None, 'tp'), may hold values from -0.125 to 0.125
Outputs:
- mixed: bfloat16 [24576, 4096], P('ctx', 'tp')
All inputs are finite; a program needn't handle non-finite values.
Results may differ from a plain program's by a relative error of at most 0.0095.
Values may be sent and summed in bfloat16 or wider, within the bound.
A program may use at most 128 MiB of HBM per device.

v0:
```python
import math
import jax
import jax.numpy as jnp
from jax import lax
from jax.sharding import Mesh
from jax.sharding import PartitionSpec as P

CTX = ("ctx_0", "ctx_1", "ctx_2")
norm_eps = 1e-06


def shifted(block, axis, distance):
    devices = range(lax.axis_size(axis))
    route = [(i - distance, i) for i in devices if i - distance in devices]
    return lax.ppermute(block, axis, route)


def sent_together(arrays, axis, split_dim, concat_dim, along):
    ends, at = ([], 0)
    for a in arrays[:-1]:
        at += a.shape[along]
        ends.append(at)
    both = jnp.concatenate(arrays, axis=along)
    return tuple(
        jnp.split(
            lax.all_to_all(both, axis, split_axis=split_dim, concat_axis=concat_dim, tiled=True),
            ends,
            axis=along,
        )
    )


def in_blocks(x, dim, peers):
    dims = x.shape
    pieces = x.reshape(*dims[:dim], peers, dims[dim] // peers, *dims[dim + 1 :])
    return jnp.moveaxis(pieces, dim, 0)


def in_order(pieces, dim):
    dims = list(pieces.shape[1:])
    dims[dim] *= pieces.shape[0]
    return jnp.moveaxis(pieces, 0, dim).reshape(dims)


def turned_blocks(pieces, axes, sequence):
    inside = pieces.shape[1:]
    out = pieces.reshape(*(lax.axis_size(a) for a in axes), *inside)
    for k in sequence:
        out = lax.all_to_all(out, axes[k], k, k, tiled=True)
    return out.reshape(-1, *inside)


def core_and_chips(x, groups, sequence, split_dim, concat_dim):
    peers = lax.axis_size(groups[0]) * lax.axis_size(groups[1])
    pieces = in_blocks(x, split_dim, peers)
    return in_order(turned_blocks(pieces, groups, sequence), concat_dim)


def angle_table(outer, inner, period):
    product = (
        jnp.arange(outer, dtype=jnp.int32)[:, None]
        * jnp.arange(inner, dtype=jnp.int32)[None, :]
        % period
    )
    phase = product.astype(jnp.float32) * (2.0 * math.pi / period)
    return (jnp.cos(phase), jnp.sin(phase))


def contract(form, left, right):
    return jnp.einsum(form, left, right, preferred_element_type=jnp.float32)


def forward_transform(signal, tables):
    cos_rows, sin_rows, cos_twist, sin_twist, cos_cols, sin_cols = tables
    first_real = contract("kn,cnm->ckm", cos_rows, signal)
    first_imag = -contract("kn,cnm->ckm", sin_rows, signal)
    turned_real = first_real * cos_twist + first_imag * sin_twist
    turned_imag = first_imag * cos_twist - first_real * sin_twist
    spec_real = contract("ckm,mj->ckj", turned_real, cos_cols) + contract(
        "ckm,mj->ckj", turned_imag, sin_cols
    )
    spec_imag = contract("ckm,mj->ckj", turned_imag, cos_cols) - contract(
        "ckm,mj->ckj", turned_real, sin_cols
    )
    return (spec_real, spec_imag)


def inverse_transform(spec_real, spec_imag, tables, period):
    cos_rows, sin_rows, cos_twist, sin_twist, cos_cols, sin_cols = tables
    back_real = contract("ckj,mj->ckm", spec_real, cos_cols) - contract(
        "ckj,mj->ckm", spec_imag, sin_cols
    )
    back_imag = contract("ckj,mj->ckm", spec_imag, cos_cols) + contract(
        "ckj,mj->ckm", spec_real, sin_cols
    )
    untwist_real = back_real * cos_twist - back_imag * sin_twist
    untwist_imag = back_imag * cos_twist + back_real * sin_twist
    signal = contract("kn,ckm->cnm", cos_rows, untwist_real) - contract(
        "kn,ckm->cnm", sin_rows, untwist_imag
    )
    return signal / period


def causal_conv(signal, kernel):
    channels = signal.shape[0]
    length = signal.shape[1]
    col_count = min(256, length)
    row_count = 2 * length // col_count
    half_rows = length // col_count
    cos_rows, sin_rows = angle_table(row_count, half_rows, row_count)
    cos_twist, sin_twist = angle_table(row_count, col_count, row_count * col_count)
    cos_cols, sin_cols = angle_table(col_count, col_count, col_count)
    tables = (cos_rows, sin_rows, cos_twist, sin_twist, cos_cols, sin_cols)
    signal_real, signal_imag = forward_transform(
        signal.astype(jnp.float32).reshape(channels, half_rows, col_count), tables
    )
    kernel_real, kernel_imag = forward_transform(
        kernel.astype(jnp.float32).reshape(channels, half_rows, col_count), tables
    )
    joint_real = signal_real * kernel_real - signal_imag * kernel_imag
    joint_imag = signal_real * kernel_imag + signal_imag * kernel_real
    result = inverse_transform(joint_real, joint_imag, tables, row_count * col_count)
    return result.reshape(channels, length)


def local(token_ids, embed_table, norm_gain, w_in, short_taps, long_filter, skip_gain, w_out):
    vocab = embed_table.shape[0]
    one_hot = (token_ids[:, None] == jnp.arange(vocab, dtype=jnp.int32)[None, :]).astype(
        jnp.bfloat16
    )
    embedded = jnp.dot(one_hot, embed_table, preferred_element_type=jnp.float32)
    scale = lax.rsqrt(jnp.mean(embedded * embedded, axis=1, keepdims=True) + norm_eps)
    normed = (embedded * scale * norm_gain).astype(jnp.bfloat16)
    width = w_in.shape[0]
    chan_part = w_in.shape[2]
    flat_proj = jnp.dot(
        normed, w_in.reshape(width, 3 * chan_part), preferred_element_type=jnp.float32
    ).astype(jnp.bfloat16)
    projected = jnp.transpose(flat_proj.reshape(-1, 3, chan_part), (1, 2, 0))
    positions = projected.shape[2]
    edge = projected[:, :, positions - 2 :]
    prior = shifted(edge, CTX, 1)
    extended = jnp.concatenate([prior, projected], axis=2).astype(jnp.float32)
    shortened = (
        short_taps[0][:, :, None] * extended[:, :, 2:]
        + short_taps[1][:, :, None] * extended[:, :, 1 : positions + 1]
        + short_taps[2][:, :, None] * extended[:, :, 0:positions]
    ).astype(jnp.bfloat16)
    query_side = shortened[0]
    key_side = shortened[1]
    value_side = shortened[2]
    local_channels = shortened.shape[1]
    groups = lax.axis_size(CTX)
    owned = local_channels // groups

    def spread(array):
        return array.reshape(groups, owned, array.shape[-1])

    first_channel = lax.axis_index(CTX) * owned
    own_skip = lax.dynamic_slice_in_dim(skip_gain, first_channel, owned)[:, None]
    product_local = (key_side.astype(jnp.float32) * value_side.astype(jnp.float32)).astype(
        jnp.bfloat16
    )
    arrived = sent_together((spread(product_local), spread(long_filter)), CTX, 0, 2, 1)
    product = arrived[0].reshape(owned, -1)
    filter_full = arrived[1].reshape(owned, -1)
    convolved = causal_conv(product, filter_full)
    outgoing = (convolved + own_skip * product.astype(jnp.float32)).astype(jnp.bfloat16)
    returned = core_and_chips(
        outgoing.reshape(1, owned, -1), (("ctx_0", "ctx_1"), "ctx_2"), (1, 0), 2, 0
    )
    returned = returned.reshape(local_channels, positions)
    gated = (query_side.astype(jnp.float32) * returned.astype(jnp.float32)).astype(jnp.bfloat16)
    width_part = w_out.shape[1]
    projected_out = jnp.dot(
        lax.all_gather(gated, "tp", axis=0, tiled=True).T, w_out, preferred_element_type=jnp.float32
    )
    residual = lax.dynamic_slice_in_dim(embedded, lax.axis_index("tp") * width_part, width_part, 1)
    return (residual + projected_out).astype(jnp.bfloat16)


def solution(mesh):
    finer = Mesh(mesh.devices.reshape(4, 4, 2, mesh.shape["tp"]), ("ctx_0", "ctx_1", "ctx_2", "tp"))
    in_specs = (
        P(CTX),
        P(),
        P(),
        P(None, None, "tp"),
        P(None, None, "tp"),
        P("tp", CTX),
        P("tp"),
        P(None, "tp"),
    )
    out_specs = P(CTX, "tp")
    return jax.shard_map(local, mesh=finer, in_specs=in_specs, out_specs=out_specs, check_vma=False)
```

profile of v0, /device:TPU:1, one launch (start us, length us, event | category | flops | bytes accessed | tf_op | source)
XLA Modules:
  0.0 231.1 jit_solution(8118276754307388498)
XLA Ops:
  6.5 8.8 %multiply_reduce_fusion = (f32[768]{0:T(1024)S(1)}, f32[768,4096]{1,0:T(8,128)}) fusion(bf16[512,4096]{1,0:T(8,128)(2,1)} %param.9, s32[768]{0:T(1024)} %param.8), kind=kOutput, calls=%fused_computation.1 | convolution fusion | flops 3227909376 | bytes 16783360 | tf_op jit(solution)/shard_map/dot_general | solution.py:131
  15.4 8.7 %copy.32 = bf16[4096,3,256]{0,2,1:T(8,128)(2,1)} copy(bf16[4096,3,256]{2,0,1:T(8,128)(2,1)} %param.11) | data formatting | bytes 12582912 | tf_op args[3]
  24.0 11.1 %fusion.19 = bf16[768,768]{0,1:T(8,128)(2,1)S(1)} fusion(bf16[4096,768]{0,1:T(8,128)(2,1)} %bitcast.149, f32[768,4096]{1,0:T(8,128)} %get-tuple-element.13, f32[4096]{0:T(1024)S(1)} %copy-done.4, f32[768]{0:T(1024)S(1)} %add_rsqrt_fusion), kind=kOutput, calls=%fused_computation.36 | convolution fusion | flops 4841865216 | bytes 20073472 | tf_op jit(solution)/shard_map/dot_general | solution.py:136
  35.2 4.9 %collective-permute-start = (bf16[3,256,2]{2,1,0:T(8,128)(2,1)S(1)}, bf16[3,256,2]{2,1,0:T(8,128)(2,1)S(1)}, u32[]{:S(2)}, u32[]{:S(2)}) collective-permute-start(bf16[3,256,2]{2,1,0:T(8,128)(2,1)S(1)} %slice.40), channel_id=1, source_target_pairs={{0,8},{8,16},{16,24},{24,32},{32,40},{40,48},{48,56},{56,64},{64,7... | collective-permute-start | bytes 9224 | tf_op jit(solution)/shard_map/ppermute | solution.py:15
  40.2 2.6 %collective-permute-done = bf16[3,256,2]{2,1,0:T(8,128)(2,1)S(1)} collective-permute-done((bf16[3,256,2]{2,1,0:T(8,128)(2,1)S(1)}, bf16[3,256,2]{2,1,0:T(8,128)(2,1)S(1)}, u32[]{:S(2)}, u32[]{:S(2)}) %collective-permute-start) | collective-permute-done | bytes 3104 | tf_op jit(solution)/shard_map/ppermute | solution.py:15
  43.4 2.0 fusion.4
  47.5 9.5 %all-to-all-start = ((bf16[32,16,768]{2,1,0:T(8,128)(2,1)}), bf16[32,16,768]{2,1,0:T(8,128)(2,1)S(1)}, u32[]{:S(2)}, u32[]{:S(2)}) async-start(bf16[32,16,768]{2,1,0:T(8,128)(2,1)} %pad_maximum_fusion), calls=%async_computation | async-start | bytes 1572864 | tf_op jit(solution)/shard_map/all_to_all | solution.py:26
  58.1 21.2 %all-to-all-done = bf16[32,16,768]{2,1,0:T(8,128)(2,1)S(1)} async-done(((bf16[32,16,768]{2,1,0:T(8,128)(2,1)}), bf16[32,16,768]{2,1,0:T(8,128)(2,1)S(1)}, u32[]{:S(2)}, u32[]{:S(2)}) %all-to-all-start) | async-done | bytes 786464 | tf_op jit(solution)/shard_map/all_to_all | solution.py:26
  82.5 1.4 fusion.54
  83.9 1.4 fusion.58
  85.3 1.4 fusion.52
  86.7 1.4 fusion.48
  88.1 1.5 convolution_subtract_fusion.1
  89.5 1.4 convolution_add_fusion.2
  91.0 1.7 convolution_add_fusion.1
  92.7 1.8 multiply_add_fusion
  100.5 1.7 fusion.26
  102.1 2.2 reshape.119
  104.4 1.6 fusion.31
  106.0 3.8 %all_to_all.28 = bf16[16,2,1,8,768]{4,3,0,2,1:T(8,128)(2,1)S(1)} all-to-all(bf16[16,2,1,8,768]{4,3,0,2,1:T(8,128)(2,1)S(1)} %copy.39), channel_id=1, replica_groups=mesh['ctx_0'=4,'ctx_1'=4,'ctx_2'=2,'tp'=8] {'ctx_2'}, dimensions={1} | all-to-all | bytes 786432 | tf_op jit(solution)/shard_map/all_to_all | solution.py:49
  109.8 16.1 %all_to_all.29 = bf16[16,2,1,8,768]{4,3,1,2,0:T(8,128)(2,1)S(1)} all-to-all(bf16[16,2,1,8,768]{4,3,1,2,0:T(8,128)(2,1)S(1)} %copy.40), channel_id=1, replica_groups=mesh['ctx_0'=4,'ctx_1'=4,'ctx_2'=2,'tp'=8] {'ctx_0','ctx_1'}, dimensions={0} | all-to-all | bytes 786432 | tf_op jit(solution)/shard_map/all_to_all | solution.py:49
  125.9 1.8 fusion.29
  127.8 91.4 %all-gather.2.cloned.1.call-done = bf16[2048,768]{1,0:T(8,128)(2,1)} async-done(((bf16[256,768]{1,0:T(8,128)(2,1)}), bf16[2048,768]{1,0:T(8,128)(2,1)}) %all-gather.2.cloned.1.call-update) | async-done | bytes 3145744 | tf_op jit(solution)/shard_map/all_gather | solution.py:176
  219.2 5.0 %add_convert_fusion = bf16[768,512]{1,0:T(8,128)(2,1)} fusion(f32[768,4096]{1,0:T(8,128)} %get-tuple-element.13, s32[]{:T(128)S(6)} %select_n.86, bf16[2048,768]{1,0:T(8,128)(2,1)} %all-gather.2.cloned.1.call-done, bf16[2048,512]{1,0:T(8,128)(2,1)S(1)} %copy-done), kind=kOutput, calls=%fused_computation.23 | convolution fusion | flops 1611399168 | bytes 7602180 | tf_op jit(solution)/shard_map/dot_general | solution.py:175
  (35 shorter events, 13.2 us)
Async XLA Ops:
  6.5 212.6 %copy-start = (bf16[2048,512]{1,0:T(8,128)(2,1)S(1)}, bf16[2048,512]{1,0:T(8,128)(2,1)}, u32[]{:S(2)}) copy-start(bf16[2048,512]{1,0:T(8,128)(2,1)} %param.15) | copy-start | bytes 6291460
  15.4 8.7 %copy-start.4 = (f32[4096]{0:T(1024)S(1)}, f32[4096]{0:T(1024)}, u32[]{:S(2)}) copy-start(f32[4096]{0:T(1024)} %param.10) | copy-start | bytes 49156
  24.0 16.1 %copy-start.3 = (f32[3,3,256]{2,1,0:T(4,128)S(1)}, f32[3,3,256]{2,1,0:T(4,128)}, u32[]{:S(2)}) copy-start(f32[3,3,256]{2,1,0:T(4,128)} %param.12) | copy-start | bytes 27652
  35.2 7.5 %collective-permute-start = (bf16[3,256,2]{2,1,0:T(8,128)(2,1)S(1)}, bf16[3,256,2]{2,1,0:T(8,128)(2,1)S(1)}, u32[]{:S(2)}, u32[]{:S(2)}) collective-permute-start(bf16[3,256,2]{2,1,0:T(8,128)(2,1)S(1)} %slice.40), channel_id=1, source_target_pairs={{0,8},{8,16},{16,24},{24,32},{32,40},{40,48},{48,56},{56,64},{64,7... | collective-permute-start | bytes 9224 | tf_op jit(solution)/shard_map/ppermute | solution.py:15
  43.3 3.2 %copy-start.2 = (bf16[256,768]{1,0:T(8,128)(2,1)S(1)}, bf16[256,768]{1,0:T(8,128)(2,1)}, u32[]{:S(2)}) copy-start(bf16[256,768]{1,0:T(8,128)(2,1)} %param.13) | copy-start | bytes 1179652
  45.4 1.1 copy-start.1
  46.6 10.7 %copy-start.5 = (f32[256]{0:T(256)S(1)}, f32[256]{0:T(256)}, u32[]{:S(2)}) copy-start(f32[256]{0:T(256)} %param.14) | copy-start | bytes 3076
  47.5 31.8 %all-to-all-start = ((bf16[32,16,768]{2,1,0:T(8,128)(2,1)}), bf16[32,16,768]{2,1,0:T(8,128)(2,1)S(1)}, u32[]{:S(2)}, u32[]{:S(2)}) async-start(bf16[32,16,768]{2,1,0:T(8,128)(2,1)} %pad_maximum_fusion), calls=%async_computation | async-start | bytes 1572864 | tf_op jit(solution)/shard_map/all_to_all | solution.py:26
  57.0 162.2 %all-gather.2.cloned.1.call-start = ((), (), s32[]{:S(2)}) async-start(), calls=%async_computation.3 | async-start | bytes 3538944 | tf_op jit(solution)/shard_map/all_gather | solution.py:176
Sparse Core Ops, SparseCore 0:
  127.9 91.2 all-gather.1
where the time goes:
time: 232 us; the launch traced here: 231 us
  waiting for transfers between devices  115 us (50%)
  matrix products  47.6 us (21%)
  blocking collectives  19.9 us (9%)
  starting transfers between devices  14.6 us (6%)
  between operations  13.6 us (6%)
  local copies, waits for them, and re-layouts  12.4 us (5%)
  other arithmetic  7.86 us (3%)
    all_gather x1, waiting for transfers between devices, local(): lax.all_gather(gated, 'tp', axis=0, tiled=True)  91.4 us
    dot_general x18, matrix products, contract(): return jnp.einsum(form, left, right, preferred_element_type=jnp.float32)  22.6 us
    all_to_all x1, waiting for transfers between devices, sent_together(): lax.all_to_all(both, axis, split_axis=split_dim, concat_axis=concat_dim,...  21.2 us
    all_to_all x2, blocking collectives, turned_blocks(): out = lax.all_to_all(out, axes[k], k, k, tiled=True)  19.9 us
    dot_general x1, matrix products, local(): jnp.dot(normed, w_in.reshape(width, 3 * chan_part), preferred_element_typ...  11.1 us
    unnamed x13, local copies, waits for them, and re-layouts  9.78 us
    all_to_all x1, starting transfers between devices, sent_together(): lax.all_to_all(both, axis, split_axis=split_dim, concat_axis=concat_dim,...  9.47 us
    dot_general x1, matrix products, local(): embedded = jnp.dot(one_hot, embed_table, preferred_element_type=jnp.float32)  8.82 us
  transfers between devices with their start and end apart: 3, of which 3 were waited for; matrix products, arithmetic and copies ran while one was open for 0% of the time, Pallas kernels for 0%

commit v1 on v0

--- a/solution.py
+++ b/solution.py
@@ -173,7 +173,11 @@
     gated = (query_side.astype(jnp.float32) * returned.astype(jnp.float32)).astype(jnp.bfloat16)
     width_part = w_out.shape[1]
     projected_out = jnp.dot(
-        lax.all_gather(gated, "tp", axis=0, tiled=True).T, w_out, preferred_element_type=jnp.float32
+        jnp.concatenate(
+            lax.all_to_all(jnp.stack([gated] * lax.axis_size("tp")), "tp", 0, 0), axis=0
+        ).T,
+        w_out,
+        preferred_element_type=jnp.float32,
     )
     residual = lax.dynamic_slice_in_dim(embedded, lax.axis_index("tp") * width_part, width_part, 1)
     return (residual + projected_out).astype(jnp.bfloat16)

time: 232 us -> 210 us (0.905)
  waiting for transfers between devices: 115 us -> 94.3 us
  between operations: 13.6 us -> 0.23 us
  starting transfers between devices: 14.6 us -> 24 us
    all_gather x1 -> x0, waiting for transfers between devices: 91.4 us -> none  [local(): lax.all_gather(gated, 'tp', axis=0, tiled=True)]
    all_to_all x0 -> x1, waiting for transfers between devices: none -> 70.5 us  [local(): lax.all_to_all(jnp.stack([gated] * lax.axis_size('tp')), 'tp', 0, 0)]
    all_to_all x0 -> x1, starting transfers between devices: none -> 9.45 us  [local(): lax.all_to_all(jnp.stack([gated] * lax.axis_size('tp')), 'tp', 0, 0)]
where the time goes in v1:
time: 210 us; the launch traced here: 207 us
  waiting for transfers between devices  94.3 us (45%)
  matrix products  47.6 us (23%)
  starting transfers between devices  24 us (11%)
  blocking collectives  19.9 us (9%)
  local copies, waits for them, and re-layouts  14.3 us (7%)
  other arithmetic  7.11 us (3%)
    all_to_all x1, waiting for transfers between devices, local(): lax.all_to_all(jnp.stack([gated] * lax.axis_size('tp')), 'tp', 0, 0)  70.5 us
    dot_general x18, matrix products, contract(): return jnp.einsum(form, left, right, preferred_element_type=jnp.float32)  22.6 us
    all_to_all x1, waiting for transfers between devices, sent_together(): lax.all_to_all(both, axis, split_axis=split_dim, concat_axis=concat_dim,...  21.2 us
    all_to_all x2, blocking collectives, turned_blocks(): out = lax.all_to_all(out, axes[k], k, k, tiled=True)  19.9 us
    dot_general x1, matrix products, local(): jnp.dot(normed, w_in.reshape(width, 3 * chan_part), preferred_element_typ...  11 us
    unnamed x13, local copies, waits for them, and re-layouts  9.8 us
    all_to_all x1, starting transfers between devices, sent_together(): lax.all_to_all(both, axis, split_axis=split_dim, concat_axis=concat_dim,...  9.66 us
    all_to_all x1, starting transfers between devices, local(): lax.all_to_all(jnp.stack([gated] * lax.axis_size('tp')), 'tp', 0, 0)  9.45 us
  transfers between devices with their start and end apart: 3, of which 3 were waited for; matrix products, arithmetic and copies ran while one was open for 0% of the time, Pallas kernels for 0%

profile of v1, /device:TPU:1, one launch (start us, length us, event | category | flops | bytes accessed | tf_op | source)
XLA Modules:
  0.0 207.4 jit_solution(4210455993650197163)
XLA Ops:
  0.0 8.8 %multiply_reduce_fusion = (f32[768]{0:T(1024)S(1)}, f32[768,4096]{1,0:T(8,128)}) fusion(bf16[512,4096]{1,0:T(8,128)(2,1)} %param.9, s32[768]{0:T(1024)} %param.8), kind=kOutput, calls=%fused_computation.1 | convolution fusion | flops 3227909376 | bytes 16783360 | tf_op jit(solution)/shard_map/dot_general | solution.py:131
  8.8 8.7 %copy.32 = bf16[4096,3,256]{0,2,1:T(8,128)(2,1)} copy(bf16[4096,3,256]{2,0,1:T(8,128)(2,1)} %param.11) | data formatting | bytes 12582912 | tf_op args[3]
  17.5 11.0 %fusion.19 = bf16[768,768]{0,1:T(8,128)(2,1)S(1)} fusion(bf16[4096,768]{0,1:T(8,128)(2,1)} %bitcast.146, f32[768,4096]{1,0:T(8,128)} %get-tuple-element.13, f32[4096]{0:T(1024)S(1)} %copy-done.4, f32[768]{0:T(1024)S(1)} %add_rsqrt_fusion), kind=kOutput, calls=%fused_computation.36 | convolution fusion | flops 4841865216 | bytes 20073472 | tf_op jit(solution)/shard_map/dot_general | solution.py:136
  28.7 4.9 %collective-permute-start = (bf16[3,256,2]{2,1,0:T(8,128)(2,1)S(1)}, bf16[3,256,2]{2,1,0:T(8,128)(2,1)S(1)}, u32[]{:S(2)}, u32[]{:S(2)}) collective-permute-start(bf16[3,256,2]{2,1,0:T(8,128)(2,1)S(1)} %slice.40), channel_id=1, source_target_pairs={{0,8},{8,16},{16,24},{24,32},{32,40},{40,48},{48,56},{56,64},{64,7... | collective-permute-start | bytes 9224 | tf_op jit(solution)/shard_map/ppermute | solution.py:15
  33.7 2.6 %collective-permute-done = bf16[3,256,2]{2,1,0:T(8,128)(2,1)S(1)} collective-permute-done((bf16[3,256,2]{2,1,0:T(8,128)(2,1)S(1)}, bf16[3,256,2]{2,1,0:T(8,128)(2,1)S(1)}, u32[]{:S(2)}, u32[]{:S(2)}) %collective-permute-start) | collective-permute-done | bytes 3104 | tf_op jit(solution)/shard_map/ppermute | solution.py:15
  36.8 2.0 fusion.4
  41.0 9.7 %all-to-all-start = ((bf16[32,16,768]{2,1,0:T(8,128)(2,1)}), bf16[32,16,768]{2,1,0:T(8,128)(2,1)S(1)}, u32[]{:S(2)}, u32[]{:S(2)}) async-start(bf16[32,16,768]{2,1,0:T(8,128)(2,1)} %pad_maximum_fusion), calls=%async_computation | async-start | bytes 1572864 | tf_op jit(solution)/shard_map/all_to_all | solution.py:26
  51.6 21.2 %all-to-all-done = bf16[32,16,768]{2,1,0:T(8,128)(2,1)S(1)} async-done(((bf16[32,16,768]{2,1,0:T(8,128)(2,1)}), bf16[32,16,768]{2,1,0:T(8,128)(2,1)S(1)}, u32[]{:S(2)}, u32[]{:S(2)}) %all-to-all-start) | async-done | bytes 786464 | tf_op jit(solution)/shard_map/all_to_all | solution.py:26
  76.0 1.4 fusion.55
  78.8 1.4 fusion.53
  80.2 1.4 fusion.49
  81.6 1.5 convolution_subtract_fusion.1
  83.0 1.4 convolution_add_fusion.2
  84.5 1.7 convolution_add_fusion.1
  86.1 1.8 multiply_add_fusion
  94.0 1.7 fusion.26
  95.6 2.2 %reshape.131 = f32[1,8,32,768]{3,2,1,0:T(8,128)} reshape(f32[8,96,256]{2,1,0:T(8,128)} %fusion.26) | data formatting | bytes 1572864 | tf_op jit(solution)/shard_map/reshape | solution.py:123
  97.9 1.6 fusion.31
  99.5 3.8 %all_to_all.33 = bf16[16,2,1,8,768]{4,3,0,2,1:T(8,128)(2,1)S(1)} all-to-all(bf16[16,2,1,8,768]{4,3,0,2,1:T(8,128)(2,1)S(1)} %copy.39), channel_id=1, replica_groups=mesh['ctx_0'=4,'ctx_1'=4,'ctx_2'=2,'tp'=8] {'ctx_2'}, dimensions={1} | all-to-all | bytes 786432 | tf_op jit(solution)/shard_map/all_to_all | solution.py:49
  103.3 16.1 %all_to_all.34 = bf16[16,2,1,8,768]{4,3,1,2,0:T(8,128)(2,1)S(1)} all-to-all(bf16[16,2,1,8,768]{4,3,1,2,0:T(8,128)(2,1)S(1)} %copy.40), channel_id=1, replica_groups=mesh['ctx_0'=4,'ctx_1'=4,'ctx_2'=2,'tp'=8] {'ctx_0','ctx_1'}, dimensions={0} | all-to-all | bytes 786432 | tf_op jit(solution)/shard_map/all_to_all | solution.py:49
  120.5 1.8 stack.5
  122.3 9.5 %all-to-all-start.3 = ((bf16[8,256,768]{2,1,0:T(8,128)(2,1)}), bf16[8,256,768]{2,1,0:T(8,128)(2,1)}, u32[]{:S(2)}, u32[]{:S(2)}) async-start(bf16[8,256,768]{2,1,0:T(8,128)(2,1)} %stack.5), calls=%async_computation.3 | async-start | bytes 6291456 | tf_op jit(solution)/shard_map/all_to_all | solution.py:177
  131.8 70.5 %all-to-all-done.3 = bf16[8,256,768]{2,1,0:T(8,128)(2,1)} async-done(((bf16[8,256,768]{2,1,0:T(8,128)(2,1)}), bf16[8,256,768]{2,1,0:T(8,128)(2,1)}, u32[]{:S(2)}, u32[]{:S(2)}) %all-to-all-start.3) | async-done | bytes 3145760 | tf_op jit(solution)/shard_map/all_to_all | solution.py:177
  202.3 5.0 %add_convert_fusion = bf16[768,512]{1,0:T(8,128)(2,1)} fusion(f32[768,4096]{1,0:T(8,128)} %get-tuple-element.13, s32[]{:T(128)S(6)} %select_n.86, bf16[2048,768]{1,0:T(8,128)(2,1)} %bitcast.28, bf16[2048,512]{1,0:T(8,128)(2,1)S(1)} %copy-done), kind=kOutput, calls=%fused_computation.23 | convolution fusion | flops 1611399168 | bytes 7602180 | tf_op jit(solution)/shard_map/dot_general | solution.py:175
  (35 shorter events, 15.4 us)
Async XLA Ops:
  0.0 202.3 %copy-start = (bf16[2048,512]{1,0:T(8,128)(2,1)S(1)}, bf16[2048,512]{1,0:T(8,128)(2,1)}, u32[]{:S(2)}) copy-start(bf16[2048,512]{1,0:T(8,128)(2,1)} %param.15) | copy-start | bytes 6291460
  8.8 8.7 %copy-start.4 = (f32[4096]{0:T(1024)S(1)}, f32[4096]{0:T(1024)}, u32[]{:S(2)}) copy-start(f32[4096]{0:T(1024)} %param.10) | copy-start | bytes 49156
  17.5 16.1 %copy-start.3 = (f32[3,3,256]{2,1,0:T(4,128)S(1)}, f32[3,3,256]{2,1,0:T(4,128)}, u32[]{:S(2)}) copy-start(f32[3,3,256]{2,1,0:T(4,128)} %param.12) | copy-start | bytes 27652
  28.7 7.5 %collective-permute-start = (bf16[3,256,2]{2,1,0:T(8,128)(2,1)S(1)}, bf16[3,256,2]{2,1,0:T(8,128)(2,1)S(1)}, u32[]{:S(2)}, u32[]{:S(2)}) collective-permute-start(bf16[3,256,2]{2,1,0:T(8,128)(2,1)S(1)} %slice.40), channel_id=1, source_target_pairs={{0,8},{8,16},{16,24},{24,32},{32,40},{40,48},{48,56},{56,64},{64,7... | collective-permute-start | bytes 9224 | tf_op jit(solution)/shard_map/ppermute | solution.py:15
  36.8 3.2 %copy-start.2 = (bf16[256,768]{1,0:T(8,128)(2,1)S(1)}, bf16[256,768]{1,0:T(8,128)(2,1)}, u32[]{:S(2)}) copy-start(bf16[256,768]{1,0:T(8,128)(2,1)} %param.13) | copy-start | bytes 1179652
  38.9 1.1 copy-start.1
  40.0 10.6 %copy-start.5 = (f32[256]{0:T(256)S(1)}, f32[256]{0:T(256)}, u32[]{:S(2)}) copy-start(f32[256]{0:T(256)} %param.14) | copy-start | bytes 3076
  41.0 31.8 %all-to-all-start = ((bf16[32,16,768]{2,1,0:T(8,128)(2,1)}), bf16[32,16,768]{2,1,0:T(8,128)(2,1)S(1)}, u32[]{:S(2)}, u32[]{:S(2)}) async-start(bf16[32,16,768]{2,1,0:T(8,128)(2,1)} %pad_maximum_fusion), calls=%async_computation | async-start | bytes 1572864 | tf_op jit(solution)/shard_map/all_to_all | solution.py:26
  122.3 80.0 %all-to-all-start.3 = ((bf16[8,256,768]{2,1,0:T(8,128)(2,1)}), bf16[8,256,768]{2,1,0:T(8,128)(2,1)}, u32[]{:S(2)}, u32[]{:S(2)}) async-start(bf16[8,256,768]{2,1,0:T(8,128)(2,1)} %stack.5), calls=%async_computation.3 | async-start | bytes 6291456 | tf_op jit(solution)/shard_map/all_to_all | solution.py:177
